TPU v7x, 32 devices: a whole 2x2x4 slice. The times are simulated.
32 devices in a mesh: groups: 2 (over y), seq: 4 (over z), role: 2 (over x), mb: 2 (over core).
Axes of the slice: x: 2, y: 2, z: 4, core: 2. Of those that a mesh axis runs over, the one named last changes fastest.
Arguments:
- queries: bfloat16 [256, 128, 576], P(('groups', 'seq'), ('role', 'mb')), parts along dimension 0, may hold values from -200 to 200
- cache: bfloat16 [256, 256, 576], P(('groups', 'seq')), parts along dimension 0, may hold values from -24 to 24
- lengths: int32 [256], P(('groups', 'seq')), parts along dimension 0, may hold values from 2 to 256
- w_uv: bfloat16 [128, 512, 128], P(('role', 'mb'), None, 'seq'), may hold values from -0.25 to 0.25
- w_o: bfloat16 [128, 128, 3584], P(('role', 'mb'), 'seq'), may hold values from -0.1875 to 0.1875
- x_in: bfloat16 [256, 3584], P('groups', 'seq'), parts along dimension 0, may hold values from -16 to 16
- norm_gain: float32 [3584], P('seq'), may hold values from 0.1 to 1.9
- w_gate: bfloat16 [8, 3584, 2048], P(('seq', 'mb'), None, 'role'), may hold values from -0.09375 to 0.09375
- w_up: bfloat16 [8, 3584, 2048], P(('seq', 'mb'), None, 'role'), may hold values from -0.09375 to 0.09375
- w_down: bfloat16 [8, 2048, 3584], P(('seq', 'mb'), 'role'), may hold values from -0.125 to 0.125
- expert_ids: int32 [256, 2], P('groups'), parts along dimension 0, may hold values from 0 to 7, all different within a row; in each aligned block of 128 rows (0 to 127, 128 to 255, ...) at most 64 rows name the same one
- gate_weights: float32 [256, 2], P('groups'), parts along dimension 0, may hold values from 0.2 to 1
- expert_slot: int32 [8], replicated, may hold values from 0 to 7, each once
Outputs:
- layer_out: bfloat16 [256, 3584], P('groups', 'seq'), parts along dimension 0
There are 2 independent parts, one for each index of `groups`. A program takes and returns all parts, laid end to end along the dimension named above; an argument that names none is the same for every part. Nothing has to cross between parts.
Inputs may be any that keep to these rules, and one draw needn't show every extreme that they name: `expert_ids`: each row names 2 different experts; over the rows of one group no expert is named more than 64 times, a bound that some block reaches. A permutation: expert e uses the weights at index expert_slot[e].
All inputs are finite; a program needn't handle non-finite values.
Results may differ from a plain program's by a relative error of at most 0.012.
Values may be sent and summed in bfloat16 or wider, within the bound.
No kernel may reach another device: no remote copies, remote signals or barrier semaphores. Data moves between devices by JAX's collectives and lax.ppermute only.
A program may use at most 128 MiB of HBM per device.

v0:
```python
import jax
import jax.numpy as jnp
from jax import lax
from jax.sharding import PartitionSpec as P

D = 3584
LAT = 512
ROPE = 64
VH = 128
ROWS = 128
CAP = 64


def per_device(
    queries,
    cache,
    lengths,
    w_uv,
    w_o,
    x_in,
    norm_gain,
    w_gate,
    w_up,
    w_down,
    expert_ids,
    gate_weights,
    expert_slot,
):
    score_scale = (VH + ROPE) ** (-0.5)
    cache_span = cache.shape[1]
    positions = jnp.arange(cache_span, dtype=jnp.int32)
    valid_mask = positions[None, :] < lengths[:, None]
    scores = (
        jnp.einsum("bhd,btd->bht", queries, cache, preferred_element_type=jnp.float32) * score_scale
    )
    scores = jnp.where(valid_mask[:, None, :], scores, -1e30)
    row_max = jnp.max(scores, axis=2)
    exp_scores = jnp.where(valid_mask[:, None, :], jnp.exp(scores - row_max[:, :, None]), 0.0)
    denominator = jnp.sum(exp_scores, axis=2)
    numerator = jnp.einsum(
        "bht,btc->bhc",
        exp_scores.astype(jnp.bfloat16),
        cache[:, :, :LAT],
        preferred_element_type=jnp.float32,
    )
    latent = (numerator / denominator[:, :, None]).astype(jnp.bfloat16)
    latent = lax.all_gather(latent, "seq", axis=0, tiled=True)
    values = jnp.einsum("bhc,hcj->bhj", latent, w_uv, preferred_element_type=jnp.float32).astype(
        jnp.bfloat16
    )
    attn_term = jnp.einsum("bhj,hjd->bd", values, w_o, preferred_element_type=jnp.float32)
    col_part = lax.psum_scatter(attn_term, "seq", scatter_dimension=1, tiled=True)
    attention = lax.psum(col_part, ("role", "mb"))
    hidden = x_in.astype(jnp.float32) + attention
    squares = lax.psum(jnp.sum(hidden * hidden, axis=1), "seq")
    normed = (hidden * lax.rsqrt(squares[:, None] / D + 1e-06) * norm_gain[None, :]).astype(
        jnp.bfloat16
    )
    seq_count = lax.axis_size("seq")
    pair_count = lax.axis_size("mb")
    pair_index = lax.axis_index("mb")
    expert_count = expert_slot.shape[0]
    expert_range = jnp.arange(expert_count, dtype=jnp.int32)
    named_mask = expert_ids[:, :, None] == expert_range[None, None, :]
    slot_of = jnp.sum(jnp.where(named_mask, expert_slot[None, None, :], 0), axis=2)
    chosen = slot_of[:, :, None] == expert_range[None, None, :]
    member = jnp.any(chosen, axis=1).astype(jnp.int32)
    gate_slot = jnp.sum(jnp.where(chosen, gate_weights[:, :, None], 0.0), axis=1)
    position = jnp.cumsum(member, axis=0) - member
    slot_range = jnp.arange(CAP, dtype=jnp.int32)
    select = (member.T[:, None, :] == 1) & (position.T[:, None, :] == slot_range[None, :, None])
    select_own = lax.dynamic_index_in_dim(
        select.reshape(seq_count, pair_count, CAP, ROWS), pair_index, 1, keepdims=False
    )
    gate_own = lax.dynamic_index_in_dim(
        gate_slot.T.reshape(seq_count, pair_count, ROWS), pair_index, 1, keepdims=False
    )
    select_half = select_own.astype(jnp.bfloat16)
    gathered = lax.all_gather(normed, "seq", axis=1, tiled=True)
    mine = lax.dynamic_index_in_dim(select_half, lax.axis_index("seq"), 0, keepdims=False)
    picked = jnp.dot(mine, gathered, preferred_element_type=jnp.float32).astype(jnp.bfloat16)
    incoming = picked[None]
    item_count = incoming.shape[1]
    rows_in = incoming.reshape(item_count, incoming.shape[2])
    gate_out = jnp.dot(rows_in, w_gate[0], preferred_element_type=jnp.float32)
    up_out = jnp.dot(rows_in, w_up[0], preferred_element_type=jnp.float32)
    activated = (jax.nn.silu(gate_out) * up_out).astype(jnp.bfloat16)
    result = jnp.dot(activated, w_down[0], preferred_element_type=jnp.float32)
    returned = lax.all_to_all(
        result[None].astype(jnp.bfloat16), "seq", split_axis=2, concat_axis=0, tiled=True
    ).astype(jnp.float32)
    mixing = select_own.astype(jnp.float32) * gate_own[:, None, :]
    partial_mix = jnp.einsum("tcb,tcd->bd", mixing, returned, precision=lax.Precision.HIGHEST)
    expert_mix = lax.psum(partial_mix.astype(jnp.bfloat16), ("role", "mb")).astype(jnp.float32)
    return (hidden + expert_mix).astype(jnp.bfloat16)


def solution(mesh):
    in_specs = (
        P(("groups", "seq"), ("role", "mb"), None),
        P(("groups", "seq"), None, None),
        P(("groups", "seq")),
        P(("role", "mb"), None, "seq"),
        P(("role", "mb"), "seq", None),
        P("groups", "seq"),
        P("seq"),
        P(("seq", "mb"), None, "role"),
        P(("seq", "mb"), None, "role"),
        P(("seq", "mb"), "role", None),
        P("groups", None),
        P("groups", None),
        P(),
    )
    out_specs = P("groups", "seq")
    return jax.shard_map(
        per_device, mesh=mesh, in_specs=in_specs, out_specs=out_specs, check_vma=False
    )
```

profile of v0, /device:TPU:0, one launch (start us, length us, event | category | flops | bytes accessed | tf_op | source)
XLA Modules:
  0.0 318.2 jit_solution(6320305931758377276)
XLA Ops:
  6.5 0.0 copy-start
  6.5 0.0 all-gather.2.cloned.1.call-start
  6.5 0.8 iota_compare_fusion.1
  7.4 0.5 copy-done
  7.9 5.5 %fusion.61 = (f32[32,32]{1,0:T(8,128)S(1)}, bf16[32,32,256]{2,1,0:T(8,128)(2,1)S(1)}) fusion(pred[32,256]{1,0:T(8,128)(4,1)S(1)} %iota_compare_fusion.1, bf16[32,32,576]{2,1,0:T(8,128)(2,1)S(1)} %copy-done, bf16[32,256,576]{1,2,0:T(8,128)(2,1)} %param.14), kind=kOutput, calls=%fused_computation.62 | convolution fusion | flops 303563008 | bytes 11153408 | tf_op jit(solution)/shard_map/sub | solution.py:38
  13.3 0.0 copy-start.2
  13.3 7.0 %divide_convert_fusion = bf16[32,32,512]{2,1,0:T(8,128)(2,1)} fusion(f32[32,32]{1,0:T(8,128)S(1)} %get-tuple-element.7, bf16[32,256,576]{1,2,0:T(8,128)(2,1)} %param.14, bf16[32,32,256]{2,1,0:T(8,128)(2,1)S(1)} %get-tuple-element.8), kind=kOutput, calls=%fused_computation.15 | convolution fusion | flops 269484032 | bytes 9965568 | tf_op jit(solution)/shard_map/bht,btc->bhc/dot_general | solution.py:40
  20.3 0.0 all-gather.2.cloned.1.call-update
  20.4 0.0 copy-start.4
  20.4 0.0 copy-start.6
  20.4 0.0 copy-start.1
  20.4 0.0 copy-start.3
  20.4 0.0 reduce-scatter.2.cloned.1.call-start
  20.5 83.5 %all-gather.2.cloned.1.call-done = bf16[128,32,512]{2,1,0:T(8,128)(2,1)} async-done(((bf16[32,32,512]{2,1,0:T(8,128)(2,1)}), bf16[128,32,512]{2,1,0:T(8,128)(2,1)}) %all-gather.2.cloned.1.call-update) | async-done | bytes 4194320 | tf_op jit(solution)/shard_map/all_gather | solution.py:47
  104.0 0.0 copy-done.2
  104.0 9.0 %convolution_bitcast_fusion = f32[128,3584]{1,0:T(8,128)} fusion(bf16[32,32,3584]{2,1,0:T(8,128)(2,1)} %param.17, bf16[32,512,32]{1,2,0:T(8,128)(2,1)S(1)} %copy-done.2, bf16[128,32,512]{2,1,0:T(8,128)(2,1)} %all-gather.2.cloned.1.call-done), kind=kOutput, calls=%fused_computation.9 | convolution fusion | flops 1073872896 | bytes 14417920 | tf_op jit(solution)/shard_map/bhj,hjd->bd/dot_general | solution.py:51
  113.0 0.0 reduce-scatter.2.cloned.1.call-update
  113.0 0.0 all-reduce.3.cloned.1.call-start
  113.1 0.0 copy-done.4
  113.1 0.0 copy-done.6
  113.1 0.1 select_reduce_fusion.1
  113.2 0.1 copy.48
  113.3 0.2 reduce_window_sum.11
  113.5 37.7 %reduce-scatter.2.cloned.1.call-done = f32[128,896]{1,0:T(8,128)} async-done(((f32[128,3584]{1,0:T(8,128)}), f32[128,896]{1,0:T(8,128)}) %reduce-scatter.2.cloned.1.call-update) | async-done | bytes 458768 | tf_op jit(solution)/shard_map/reduce_scatter | solution.py:52
  151.2 0.0 all-reduce.3.cloned.1.call-update
  151.3 0.1 copy.49
  151.4 0.1 fusion.47
  151.5 34.2 %all-reduce.3.cloned.1.call-done = f32[128,896]{1,0:T(8,128)} async-done(((f32[128,896]{1,0:T(8,128)}), f32[128,896]{1,0:T(8,128)}) %all-reduce.3.cloned.1.call-update) | async-done | bytes 458768 | tf_op jit(solution)/shard_map/psum | solution.py:53
  185.7 0.0 copy-done.1
  185.7 1.2 multiply_reduce_fusion
  186.9 11.8 %psum.22 = f32[128]{0:T(128)S(1)} all-reduce(f32[128]{0:T(128)S(1)} %multiply_reduce_fusion), channel_id=1, replica_groups=mesh['groups'=2,'seq'=4,'role'=2,'mb'=2] {'seq'}, use_global_device_ids=true, to_apply=%region_9.10 | all-reduce | flops 128 | bytes 1024 | tf_op jit(solution)/shard_map/psum | solution.py:55
  198.7 0.0 copy-done.3
  198.7 1.1 multiply_convert_fusion
  199.8 18.0 %all_gather.7 = bf16[128,3584]{1,0:T(8,128)(2,1)S(1)} all-gather(bf16[128,896]{1,0:T(8,128)(2,1)S(1)} %multiply_convert_fusion), channel_id=1, replica_groups=mesh['groups'=2,'seq'=4,'role'=2,'mb'=2] {'seq'}, dimensions={1}, use_global_device_ids=true | all-gather | bytes 1146880 | tf_op jit(solution)/shard_map/all_gather | solution.py:79
  217.8 0.3 convolution_convert_fusion
  218.1 4.5 %fusion.7 = f32[64,1024]{1,0:T(8,128)S(1)} fusion(bf16[64,3584]{1,0:T(8,128)(2,1)S(1)} %convolution_convert_fusion, bf16[1,3584,1024]{2,1,0:T(8,128)(2,1)} %param.20), kind=kOutput, calls=%fused_computation.7 | convolution fusion | flops 469762048 | bytes 8060928 | tf_op jit(solution)/shard_map/dot_general | solution.py:85
  222.6 8.6 %fusion.12 = bf16[1,64,3584]{2,1,0:T(8,128)(2,1)} fusion(bf16[1,1024,3584]{2,1,0:T(8,128)(2,1)} %param.22, bf16[64,3584]{1,0:T(8,128)(2,1)S(1)} %convolution_convert_fusion, bf16[1,3584,1024]{2,1,0:T(8,128)(2,1)} %param.21, f32[64,1024]{1,0:T(8,128)S(1)} %fusion.7), kind=kOutput, calls=%fused_computation.12 | convolution fusion | flops 940146688 | bytes 15859712 | tf_op jit(solution)/shard_map/dot_general | solution.py:88
  231.2 0.0 copy-start.5
  231.2 4.2 %copy.53 = bf16[1,64,3584]{1,0,2:T(2,128)(2,1)S(1)} copy(bf16[1,64,3584]{2,1,0:T(8,128)(2,1)} %fusion.12) | data formatting | bytes 917504 | tf_op jit(solution)/shard_map/convert_element_type | solution.py:90
  235.4 0.5 broadcast.36
  236.0 20.6 %reduce = bf16[3584,64]{1,0:T(8,128)(2,1)} reduce(bf16[3584,1,64]{2,1,0:T(2,128)(2,1)S(1)} %bitcast.64, bf16[]{:T(256)} %broadcast.36), dimensions={1}, to_apply=%bitcast.54.reduce_sub_computation | reduce | bytes 917506
  256.6 2.8 reshape.46
  259.4 4.1 %all-to-all-start = ((bf16[4,2,28672]{2,1,0:T(2,128)(2,1)}), bf16[4,2,28672]{2,1,0:T(2,128)(2,1)}, u32[]{:S(2)}, u32[]{:S(2)}) async-start(bf16[4,2,28672]{2,1,0:T(2,128)(2,1)} %reshape.46), calls=%async_computation.1 | async-start | bytes 917504 | tf_op jit(solution)/shard_map/all_to_all | solution.py:89
  263.6 0.0 all-reduce.5.cloned.1.call-start
  263.6 0.0 copy-done.5
  263.6 9.6 %all-to-all-done = bf16[4,2,28672]{2,1,0:T(2,128)(2,1)} async-done(((bf16[4,2,28672]{2,1,0:T(2,128)(2,1)}), bf16[4,2,28672]{2,1,0:T(2,128)(2,1)}, u32[]{:S(2)}, u32[]{:S(2)}) %all-to-all-start) | async-done | bytes 458784 | tf_op jit(solution)/shard_map/all_to_all | solution.py:89
  273.2 2.4 reshape.47
  275.6 1.0 copy.58
  276.7 1.5 copy.55
  278.2 1.1 fusion.24
  279.3 0.0 all-reduce.5.cloned.1.call-update
  279.3 30.5 %all-reduce.5.cloned.1.call-done = bf16[128,896]{1,0:T(8,128)(2,1)} async-done(((bf16[128,896]{1,0:T(8,128)(2,1)}), bf16[128,896]{1,0:T(8,128)(2,1)}) %all-reduce.5.cloned.1.call-update) | async-done | bytes 229392 | tf_op jit(solution)/shard_map/psum | solution.py:94
  309.8 1.9 add_convert_fusion
  (10 shorter events, 0.1 us)
Async XLA Ops:
  6.5 1.3 copy-start
  6.5 97.4 %all-gather.2.cloned.1.call-start = ((), (), s32[]{:S(2)}) async-start(), calls=%async_computation.2 | async-start | bytes 5242880 | tf_op jit(solution)/shard_map/all_gather | solution.py:47
  13.3 90.6 %copy-start.2 = (bf16[32,512,32]{1,2,0:T(8,128)(2,1)S(1)}, bf16[32,512,32]{1,2,0:T(8,128)(2,1)}, u32[]{:S(2)}) copy-start(bf16[32,512,32]{1,2,0:T(8,128)(2,1)} %param.16) | copy-start | bytes 3145732
  20.4 92.7 %copy-start.4 = (s32[128,2]{0,1:T(2,128)S(1)}, s32[128,2]{0,1:T(2,128)}, u32[]{:S(2)}) copy-start(s32[128,2]{0,1:T(2,128)} %param.23) | copy-start | bytes 3076
  20.4 92.7 %copy-start.6 = (s32[8]{0:T(128)S(1)}, s32[8]{0:T(128)}, u32[]{:S(2)}) copy-start(s32[8]{0:T(128)} %param.25) | copy-start | bytes 100
  20.4 165.3 %copy-start.1 = (bf16[128,896]{1,0:T(8,128)(2,1)S(1)}, bf16[128,896]{1,0:T(8,128)(2,1)}, u32[]{:S(2)}) copy-start(bf16[128,896]{1,0:T(8,128)(2,1)} %param.18) | copy-start | bytes 688132
  20.4 178.3 %copy-start.3 = (f32[896]{0:T(1024)S(1)}, f32[896]{0:T(1024)}, u32[]{:S(2)}) copy-start(f32[896]{0:T(1024)} %param.19) | copy-start | bytes 10756
  20.4 130.8 %reduce-scatter.2.cloned.1.call-start = ((), (), s32[]{:S(2)}) async-start(), calls=%async_computation.3 | async-start | bytes 2293760 | tf_op jit(solution)/shard_map/reduce_scatter | solution.py:52
  113.0 72.7 %all-reduce.3.cloned.1.call-start = ((), (), s32[]{:S(2)}) async-start(), calls=%async_computation.4 | async-start | bytes 917504 | tf_op jit(solution)/shard_map/psum | solution.py:53
  231.2 32.4 %copy-start.5 = (f32[128,2]{0,1:T(2,128)S(1)}, f32[128,2]{0,1:T(2,128)}, u32[]{:S(2)}) copy-start(f32[128,2]{0,1:T(2,128)} %param.24) | copy-start | bytes 3076
  259.4 13.8 %all-to-all-start = ((bf16[4,2,28672]{2,1,0:T(2,128)(2,1)}), bf16[4,2,28672]{2,1,0:T(2,128)(2,1)}, u32[]{:S(2)}, u32[]{:S(2)}) async-start(bf16[4,2,28672]{2,1,0:T(2,128)(2,1)} %reshape.46), calls=%async_computation.1 | async-start | bytes 917504 | tf_op jit(solution)/shard_map/all_to_all | solution.py:89
  263.6 46.3 %all-reduce.5.cloned.1.call-start = ((), (), s32[]{:S(2)}) async-start(), calls=%async_computation.5 | async-start | bytes 458752 | tf_op jit(solution)/shard_map/psum | solution.py:94
Sparse Core Ops, SparseCore 0:
  20.5 83.4 all-gather.1
  113.1 37.9 reduce-scatter.1
  153.5 32.1 all-reduce.2
  279.5 30.3 all-reduce.4
where the time goes:
time: 319 us; the launch traced here: 318 us
  waiting for transfers between devices  196 us (61%)
  matrix products  36 us (11%)
  blocking collectives  29.8 us (9%)
  other arithmetic  26 us (8%)
  local copies, waits for them, and re-layouts  13.4 us (4%)
  between operations  13.3 us (4%)
  starting transfers between devices  4.25 us (1%)
    all_gather x1, waiting for transfers between devices, per_device(): latent = lax.all_gather(latent, 'seq', axis=0, tiled=True)  83.5 us
    reduce_scatter x1, waiting for transfers between devices, per_device(): lax.psum_scatter(attn_term, 'seq', scatter_dimension=1, tiled=True)  37.7 us
    psum x1, waiting for transfers between devices, per_device(): attention = lax.psum(col_part, ('role', 'mb'))  34.2 us
    psum x1, waiting for transfers between devices, per_device(): lax.psum(partial_mix.astype(jnp.bfloat16), ('role', 'mb'))  30.5 us
    unnamed x1, other arithmetic  20.6 us
    all_gather x1, blocking collectives, per_device(): gathered = lax.all_gather(normed, 'seq', axis=1, tiled=True)  18 us
    psum x1, blocking collectives, per_device(): squares = lax.psum(jnp.sum(hidden * hidden, axis=1), 'seq')  11.8 us
    all_to_all x1, waiting for transfers between devices, per_device(): lax.all_to_all(result[None].astype(jnp.bfloat16), 'seq', split_axis=2, co...  9.55 us
  transfers between devices with their start and end apart: 5, of which 5 were waited for; matrix products, arithmetic and copies ran while one was open for 0% of the time, Pallas kernels for 0%

commit v1 on v0

v1 whole, which is shorter than its diff:
```python
import jax
import jax.numpy as jnp
from jax import lax
from jax.sharding import PartitionSpec as P

CAP = 64
EPS = 1e-06
BF = jnp.bfloat16
F32 = jnp.float32


def swap(value, axis, offset):
    count = lax.axis_size(axis)
    return lax.ppermute(value, axis, [(i, i ^ offset) for i in range(count)])


def block(value, index, axis=0):
    return lax.dynamic_index_in_dim(value, index, axis, keepdims=False)


def in_order(parts, me):
    return jnp.stack([lax.select_n(me ^ s, *parts) if len(parts) > 2
                      else jnp.where((me ^ s) == 0, parts[0], parts[1])
                      for s in range(len(parts))])


def sum_scatter(value, axis):
    me, count = lax.axis_index(axis), lax.axis_size(axis)
    sent = [swap(block(value, me ^ k).astype(BF), axis, k) for k in range(1, count)]
    total = block(value, me)
    for part in sent:
        total = total + part.astype(F32)
    return total


def gather_parts(value, axis):
    return [value] + [swap(value, axis, k) for k in range(1, lax.axis_size(axis))]


def attend(queries, cache, lengths, latent_width, score_scale):
    positions = jnp.arange(cache.shape[1], dtype=jnp.int32)
    valid = positions[None, :] < lengths[:, None]
    scores = jnp.einsum("bhd,btd->bht", queries, cache, preferred_element_type=F32) * score_scale
    scores = jnp.where(valid[:, None, :], scores, -1e30)
    row_max = jnp.max(scores, axis=2)
    exp_scores = jnp.where(valid[:, None, :], jnp.exp(scores - row_max[:, :, None]), 0.0)
    denominator = jnp.sum(exp_scores, axis=2)
    numerator = jnp.einsum(
        "bht,btc->bhc", exp_scores.astype(BF), cache[:, :, :latent_width], preferred_element_type=F32
    )
    return (numerator / denominator[:, :, None]).astype(BF)


def per_device(
    queries, cache, lengths, w_uv, w_o, x_in, norm_gain, w_gate, w_up, w_down,
    expert_ids, gate_weights, expert_slot,
):
    groups, seqs = lax.axis_size("groups"), lax.axis_size("seq")
    roles, cores = lax.axis_size("role"), lax.axis_size("mb")
    g, z = lax.axis_index("groups"), lax.axis_index("seq")
    x, c = lax.axis_index("role"), lax.axis_index("mb")
    heads, latent_width, width = w_uv.shape
    own_rows = queries.shape[0]
    rows, feats = x_in.shape
    model = feats * seqs
    near = 1
    while near * near < seqs:
        near *= 2
    far = seqs // near

    part = block(w_uv.reshape(groups, heads // groups, latent_width, width), g)
    foreign_maps = []
    for k in range(1, far):
        fetched = swap(part, "seq", k * near)
        both = in_order(gather_parts(fetched, "groups"), g)
        foreign_maps.append(both.reshape(heads, latent_width, width))

    score_scale = (width * seqs + queries.shape[2] - latent_width) ** (-0.5)
    latent = attend(queries, cache, lengths, latent_width, score_scale)
    latents = jnp.stack([latent] + [swap(latent, "seq", k) for k in range(1, near)])
    latents = latents.reshape(near * own_rows, heads, latent_width)

    def project(value_map):
        return jnp.einsum("bhc,hcj->bhj", latents, value_map, preferred_element_type=F32).astype(BF)

    given = [swap(project(m), "seq", (k + 1) * near) for k, m in enumerate(foreign_maps)]
    pieces = []
    for value in [project(w_uv)] + given:
        value = value.reshape(near, own_rows, heads * width)
        pieces += [value[i] for i in range(near)]
    values = in_order(pieces, z).reshape(rows, heads * width)
    attn = jnp.dot(values, w_o.reshape(heads * width, model), preferred_element_type=F32)

    quarter = rows // (roles * cores)
    attn = attn.reshape(roles, cores, quarter, model).transpose(1, 0, 2, 3)
    attn = sum_scatter(attn, "mb")
    attn = sum_scatter(attn, "role")
    attn = sum_scatter(attn.reshape(quarter, seqs, feats).transpose(1, 0, 2), "seq")
    x_own = block(x_in.reshape(roles * cores, quarter, feats), x * cores + c)
    hidden = x_own.astype(F32) + attn

    squares = jnp.sum(hidden * hidden, axis=1, keepdims=True)
    high = squares.astype(BF)
    low = (squares - high.astype(F32)).astype(BF)
    pad = jnp.zeros((quarter, 126), BF)
    packed = jnp.concatenate([(hidden * norm_gain[None, :]).astype(BF), high, low, pad], axis=1)
    parts = gather_parts(packed, "seq")
    total = sum(p[:, feats].astype(F32) + p[:, feats + 1].astype(F32) for p in parts)
    scale = lax.rsqrt(total / model + EPS)
    ordered = in_order([p[:, :feats] for p in parts], z)
    normed = (ordered.astype(F32) * scale[None, :, None]).astype(BF)
    normed = normed.transpose(1, 0, 2).reshape(quarter, model)
    normed = jnp.stack(gather_parts(normed, "role"))
    normed = jnp.stack(gather_parts(normed, "mb"))

    experts = expert_slot.shape[0]
    slot = z * cores + c
    mine_slot = jnp.sum(
        jnp.where(expert_ids[:, :, None] == jnp.arange(experts, dtype=jnp.int32), expert_slot, 0), axis=2
    ) == slot
    member = jnp.any(mine_slot, axis=1)
    gate_row = jnp.sum(jnp.where(mine_slot, gate_weights, 0.0), axis=1)
    lower = (jnp.arange(rows)[:, None] > jnp.arange(rows)[None, :]).astype(F32)
    position = jnp.dot(lower, member.astype(F32)[:, None])[:, 0].astype(jnp.int32)
    select = member[None, :] & (position[None, :] == jnp.arange(CAP, dtype=jnp.int32)[:, None])
    slot_gate = jnp.sum(jnp.where(select, gate_row[None, :], 0.0), axis=1, keepdims=True)
    blocks = select.reshape(CAP, roles, cores, quarter)
    picker = jnp.stack([
        jnp.stack([block(block(blocks, c ^ j, 2), x ^ i, 1) for i in range(roles)], axis=1)
        for j in range(cores)
    ], axis=1).reshape(CAP, rows).astype(BF)

    picked = jnp.dot(picker, normed.reshape(rows, model), preferred_element_type=F32).astype(BF)
    gate_out = jnp.dot(picked, w_gate[0], preferred_element_type=F32)
    up_out = jnp.dot(picked, w_up[0], preferred_element_type=F32)
    activated = (jax.nn.silu(gate_out) * up_out).astype(BF)
    result = jnp.dot(activated, w_down[0], preferred_element_type=F32)
    result = (result * slot_gate).astype(BF)

    spread = blocks.transpose(2, 1, 3, 0).reshape(cores, roles * quarter, CAP).astype(BF)
    sent = [
        swap(jnp.dot(block(spread, c ^ k), result, preferred_element_type=F32).astype(BF), "mb", k)
        for k in range(1, cores)
    ]
    mixed = jnp.dot(block(spread, c), result, preferred_element_type=F32)
    for p in sent:
        mixed = mixed + p.astype(F32)
    mixed = sum_scatter(mixed.reshape(roles * quarter, seqs, feats).transpose(1, 0, 2), "seq")
    mixed = mixed.reshape(roles, quarter, feats)
    at_own = jnp.arange(roles)[:, None, None] == x
    mixed = jnp.where(at_own, mixed + hidden[None], mixed).astype(BF)
    shares = gather_parts(mixed, "role")
    shares = shares if roles == 2 else in_order(shares, x)
    out = sum(p.astype(F32) for p in shares).astype(BF)
    out = in_order(gather_parts(out, "mb"), c)
    return out.transpose(1, 0, 2, 3).reshape(rows, feats)


def solution(mesh):
    in_specs = (
        P(("groups", "seq"), ("role", "mb"), None),
        P(("groups", "seq"), None, None),
        P(("groups", "seq")),
        P(("role", "mb"), None, "seq"),
        P(("role", "mb"), "seq", None),
        P("groups", "seq"),
        P("seq"),
        P(("seq", "mb"), None, "role"),
        P(("seq", "mb"), None, "role"),
        P(("seq", "mb"), "role", None),
        P("groups", None),
        P("groups", None),
        P(),
    )
    out_specs = P("groups", "seq")
    return jax.shard_map(
        per_device, mesh=mesh, in_specs=in_specs, out_specs=out_specs, check_vma=False
    )
```

time: 319 us -> 148 us (0.46)
  waiting for transfers between devices: 196 us -> 74.5 us
  blocking collectives: 29.8 us -> 0 us
  starting transfers between devices: 4.25 us -> 27.6 us
  other arithmetic: 26 us -> 6.52 us
  between operations: 13.3 us -> 0.45 us
  local copies, waits for them, and re-layouts: 13.4 us -> 6 us
    all_gather x1 -> x0, waiting for transfers between devices: 83.5 us -> none  [per_device(): latent = lax.all_gather(latent, 'seq', axis=0, tiled=True)]
    ppermute x0 -> x20, waiting for transfers between devices: none -> 74.5 us  [swap(): return lax.ppermute(value, axis, [(i, i ^ offset) for i in range(count)])]
    psum x2 -> x0, waiting for transfers between devices: 64.7 us -> none  [the longest x1 34.2 us: per_device(): attention = lax.psum(col_part, ('role', 'mb'))]
    reduce_scatter x1 -> x0, waiting for transfers between devices: 37.7 us -> none  [per_device(): lax.psum_scatter(attn_term, 'seq', scatter_dimension=1, tiled=True)]
    ppermute x0 -> x20, starting transfers between devices: none -> 27.6 us  [swap(): return lax.ppermute(value, axis, [(i, i ^ offset) for i in range(count)])]
    unnamed x1 -> x0, other arithmetic: 20.6 us -> none
    all_gather x1 -> x0, blocking collectives: 18 us -> none  [per_device(): gathered = lax.all_gather(normed, 'seq', axis=1, tiled=True)]
    psum x1 -> x0, blocking collectives: 11.8 us -> none  [per_device(): squares = lax.psum(jnp.sum(hidden * hidden, axis=1), 'seq')]
  transfers between devices with their start and end apart: 5 -> 20, of which waited for: 5 -> 17; matrix products, arithmetic and copies ran while one was open for 0% -> 12% of each run, Pallas kernels for 0% -> 0%
where the time goes in v1:
time: 148 us
  waiting for transfers between devices  74.5 us (50%)
  matrix products  33 us (22%)
  starting transfers between devices  27.6 us (19%)
  other arithmetic  6.52 us (4%)
  local copies, waits for them, and re-layouts  6 us (4%)
    ppermute x20, waiting for transfers between devices, swap(): return lax.ppermute(value, axis, [(i, i ^ offset) for i in range(count)])  74.5 us
    ppermute x20, starting transfers between devices, swap(): return lax.ppermute(value, axis, [(i, i ^ offset) for i in range(count)])  27.6 us
    dot_general x1, matrix products, per_device(): result = jnp.dot(activated, w_down[0], preferred_element_type=F32)  8.14 us
    dot_general x1, matrix products, attend(): jnp.einsum('bht,btc->bhc', exp_scores.astype(BF), cache[:, :, :latent_wid...  5.93 us
    sub x1, matrix products, attend(): scores - row_max[:, :, None]  5.48 us
    dot_general x1, matrix products, per_device(): gate_out = jnp.dot(picked, w_gate[0], preferred_element_type=F32)  4.47 us
    dot_general x1, matrix products, per_device(): jnp.dot(values, w_o.reshape(heads * width, model), preferred_element_type...  4.22 us
    dot_general x2, matrix products, project(): jnp.einsum('bhc,hcj->bhj', latents, value_map, preferred_element_type=F32)  3.82 us
  transfers between devices with their start and end apart: 20, of which 17 were waited for; matrix products, arithmetic and copies ran while one was open for 12% of the time, Pallas kernels for 0%

profile of v1, /device:TPU:0, one launch (start us, length us, event | category | flops | bytes accessed | tf_op | source)
XLA Modules:
  0.0 148.1 jit_solution(10125680161378757996)
XLA Ops:
  0.0 2.0 %dynamic-slice_bitcast_fusion = bf16[16,512,32]{1,2,0:T(8,128)(2,1)} fusion(bf16[2,16,512,32]{2,3,1,0:T(8,128)(2,1)} %bitcast.182, s32[]{:T(128)S(6)} %select_n.431), kind=kLoop, calls=%fused_computation.42 | loop fusion | bytes 1048580 | tf_op jit(solution)/shard_map/jit(dynamic_index_in_dim)/squeeze | solution.py:18
  2.0 4.1 %collective-permute-start.1 = (bf16[16,512,32]{1,2,0:T(8,128)(2,1)}, bf16[16,512,32]{1,2,0:T(8,128)(2,1)}, u32[]{:S(2)}, u32[]{:S(2)}) collective-permute-start(bf16[16,512,32]{1,2,0:T(8,128)(2,1)} %dynamic-slice_bitcast_fusion), channel_id=1, source_target_pairs={{0,8},{4,12},{8,0},{12,4},{1,9},{5,13},{9,1},{13,5},{2,10},{6,14},... | collective-permute-start | bytes 1572872 | tf_op jit(solution)/shard_map/ppermute | solution.py:14
  6.0 0.7 iota_compare_fusion.5
  6.8 5.5 %fusion.96 = (f32[32,32]{1,0:T(8,128)S(1)}, bf16[32,32,256]{2,1,0:T(8,128)(2,1)S(1)}) fusion(pred[32,256]{1,0:T(8,128)(4,1)S(1)} %iota_compare_fusion.5, bf16[32,32,576]{2,1,0:T(8,128)(2,1)S(1)} %copy-done, bf16[32,256,576]{1,2,0:T(8,128)(2,1)} %param.14), kind=kOutput, calls=%fused_computation.146 | convolution fusion | flops 303563008 | bytes 11153408 | tf_op jit(solution)/shard_map/sub | solution.py:46
  12.3 5.9 %divide_convert_fusion = bf16[32,32,512]{2,1,0:T(8,128)(2,1)S(1)} fusion(f32[32,32]{1,0:T(8,128)S(1)} %get-tuple-element.32, bf16[32,256,576]{1,2,0:T(8,128)(2,1)} %param.14, bf16[32,32,256]{2,1,0:T(8,128)(2,1)S(1)} %get-tuple-element.33), kind=kOutput, calls=%fused_computation.15 | convolution fusion | flops 269484032 | bytes 9965568 | tf_op jit(solution)/shard_map/bht,btc->bhc/dot_general | solution.py:48
  18.2 1.6 %collective-permute-start = (bf16[32,32,512]{2,1,0:T(8,128)(2,1)S(1)}, bf16[32,32,512]{2,1,0:T(8,128)(2,1)S(1)}, u32[]{:S(2)}, u32[]{:S(2)}) collective-permute-start(bf16[32,32,512]{2,1,0:T(8,128)(2,1)S(1)} %divide_convert_fusion), channel_id=1, source_target_pairs={{0,4},{4,0},{8,12},{12,8},{1,5},{5,1},{9,13},{13,9},{2,6},{6,2},{1... | collective-permute-start | bytes 3145736 | tf_op jit(solution)/shard_map/ppermute | solution.py:14
  19.8 9.8 %collective-permute-done.1 = bf16[16,512,32]{1,2,0:T(8,128)(2,1)} collective-permute-done((bf16[16,512,32]{1,2,0:T(8,128)(2,1)}, bf16[16,512,32]{1,2,0:T(8,128)(2,1)}, u32[]{:S(2)}, u32[]{:S(2)}) %collective-permute-start.1) | collective-permute-done | bytes 524320 | tf_op jit(solution)/shard_map/ppermute | solution.py:14
  29.6 1.6 %collective-permute-start.2 = (bf16[16,512,32]{1,2,0:T(8,128)(2,1)}, bf16[16,512,32]{1,2,0:T(8,128)(2,1)}, u32[]{:S(2)}, u32[]{:S(2)}) collective-permute-start(bf16[16,512,32]{1,2,0:T(8,128)(2,1)} %collective-permute-done.1), channel_id=1, source_target_pairs={{0,16},{16,0},{1,17},{17,1},{2,18},{18,2},{3,19},{19,3},{4,20},{20... | collective-permute-start | bytes 1572872 | tf_op jit(solution)/shard_map/ppermute | solution.py:14
  31.2 11.8 %collective-permute-done.2 = bf16[16,512,32]{1,2,0:T(8,128)(2,1)} collective-permute-done((bf16[16,512,32]{1,2,0:T(8,128)(2,1)}, bf16[16,512,32]{1,2,0:T(8,128)(2,1)}, u32[]{:S(2)}, u32[]{:S(2)}) %collective-permute-start.2) | collective-permute-done | bytes 524320 | tf_op jit(solution)/shard_map/ppermute | solution.py:14
  43.0 1.3 select_bitcast_fusion.1
  44.3 7.5 %collective-permute-done = bf16[32,32,512]{2,1,0:T(8,128)(2,1)S(1)} collective-permute-done((bf16[32,32,512]{2,1,0:T(8,128)(2,1)S(1)}, bf16[32,32,512]{2,1,0:T(8,128)(2,1)S(1)}, u32[]{:S(2)}, u32[]{:S(2)}) %collective-permute-start) | collective-permute-done | bytes 1048608 | tf_op jit(solution)/shard_map/ppermute | solution.py:14
  51.9 0.2 pad_maximum_fusion
  52.1 1.3 fusion.30
  53.4 1.6 %collective-permute-start.3 = (bf16[64,32,32]{0,2,1:T(8,128)(2,1)S(1)}, bf16[64,32,32]{0,2,1:T(8,128)(2,1)S(1)}, u32[]{:S(2)}, u32[]{:S(2)}) collective-permute-start(bf16[64,32,32]{0,2,1:T(8,128)(2,1)S(1)} %fusion.30), channel_id=1, source_target_pairs={{0,8},{4,12},{8,0},{12,4},{1,9},{5,13},{9,1},{13,5},{2,10},{6,14},... | collective-permute-start | bytes 393224 | tf_op jit(solution)/shard_map/ppermute | solution.py:14
  54.9 2.5 %fusion.33 = bf16[64,32,32]{0,2,1:T(8,128)(2,1)S(1)} fusion(bf16[32,512,32]{1,2,0:T(8,128)(2,1)} %param.16, bf16[64,32,512]{2,1,0:T(8,128)(2,1)S(1)} %bitcast.170), kind=kOutput, calls=%fused_computation.28 | convolution fusion | flops 67174400 | bytes 3276800 | tf_op jit(solution)/shard_map/bhc,hcj->bhj/dot_general | solution.py:84
  57.5 10.7 %collective-permute-done.3 = bf16[64,32,32]{0,2,1:T(8,128)(2,1)S(1)} collective-permute-done((bf16[64,32,32]{0,2,1:T(8,128)(2,1)S(1)}, bf16[64,32,32]{0,2,1:T(8,128)(2,1)S(1)}, u32[]{:S(2)}, u32[]{:S(2)}) %collective-permute-start.3) | collective-permute-done | bytes 131104 | tf_op jit(solution)/shard_map/ppermute | solution.py:14
  68.1 0.2 select_select_fusion.2
  68.3 0.1 copy.101
  68.5 0.1 copy.99
  68.6 0.2 select_select_fusion.3
  68.9 0.1 copy.98
  69.1 4.2 %fusion.97 = f32[2,2,32,3584]{3,2,1,0:T(8,128)S(1)} fusion(bf16[2,2,32,1024]{3,2,1,0:T(8,128)(2,1)S(1)} %bitcast.173, bf16[1024,3584,1,1]{1,0,3,2:T(8,128)(2,1)} %bitcast.168), kind=kOutput, calls=%fused_computation.147 | convolution fusion | flops 939524096 | bytes 9437184 | tf_op jit(solution)/shard_map/dot_general | solution.py:92
  73.5 1.9 %collective-permute-done.4 = bf16[2,32,3584]{2,1,0:T(8,128)(2,1)} collective-permute-done((bf16[2,32,3584]{2,1,0:T(8,128)(2,1)S(1)}, bf16[2,32,3584]{2,1,0:T(8,128)(2,1)}, u32[]{:S(2)}, u32[]{:S(2)}) %collective-permute-start.4) | collective-permute-done | bytes 458784 | tf_op jit(solution)/shard_map/ppermute | solution.py:14
  75.5 1.1 bitcast_add_fusion
  76.6 1.6 %collective-permute-start.5 = (bf16[32,3584]{1,0:T(8,128)(2,1)S(1)}, bf16[32,3584]{1,0:T(8,128)(2,1)S(1)}, u32[]{:S(2)}, u32[]{:S(2)}) collective-permute-start(bf16[32,3584]{1,0:T(8,128)(2,1)S(1)} %fusion.58), channel_id=1, source_target_pairs={{0,2},{2,0},{1,3},{3,1},{4,6},{6,4},{5,7},{7,5},{8,10},{10,8},{9,1... | collective-permute-start | bytes 688136 | tf_op jit(solution)/shard_map/ppermute | solution.py:14
  78.4 5.9 %collective-permute-done.5 = bf16[32,3584]{1,0:T(8,128)(2,1)S(1)} collective-permute-done((bf16[32,3584]{1,0:T(8,128)(2,1)S(1)}, bf16[32,3584]{1,0:T(8,128)(2,1)S(1)}, u32[]{:S(2)}, u32[]{:S(2)}) %collective-permute-start.5) | collective-permute-done | bytes 229408 | tf_op jit(solution)/shard_map/ppermute | solution.py:14
  84.4 0.2 reshape.393
  84.5 0.3 constant_dynamic-slice_fusion.6
  85.0 3.0 %collective-permute-start.7 = (bf16[32,896]{1,0:T(8,128)(2,1)S(1)}, bf16[32,896]{1,0:T(8,128)(2,1)S(1)}, u32[]{:S(2)}, u32[]{:S(2)}) collective-permute-start(bf16[32,896]{1,0:T(8,128)(2,1)S(1)} %bitcast.189), channel_id=1, source_target_pairs={{0,8},{4,12},{8,0},{12,4},{1,9},{5,13},{9,1},{13,5},{2,10},{6,14},... | collective-permute-start | bytes 172040 | tf_op jit(solution)/shard_map/ppermute | solution.py:14
  88.0 1.5 %collective-permute-start.8 = (bf16[32,896]{1,0:T(8,128)(2,1)S(1)}, bf16[32,896]{1,0:T(8,128)(2,1)S(1)}, u32[]{:S(2)}, u32[]{:S(2)}) collective-permute-start(bf16[32,896]{1,0:T(8,128)(2,1)S(1)} %bitcast.190), channel_id=1, source_target_pairs={{0,12},{4,8},{8,4},{12,0},{1,13},{5,9},{9,5},{13,1},{2,14},{6,10},... | collective-permute-start | bytes 172040 | tf_op jit(solution)/shard_map/ppermute | solution.py:14
  89.6 1.3 collective-permute-done.7
  90.9 3.1 %collective-permute-done.8 = bf16[32,896]{1,0:T(8,128)(2,1)S(1)} collective-permute-done((bf16[32,896]{1,0:T(8,128)(2,1)S(1)}, bf16[32,896]{1,0:T(8,128)(2,1)S(1)}, u32[]{:S(2)}, u32[]{:S(2)}) %collective-permute-start.8) | collective-permute-done | bytes 57376 | tf_op jit(solution)/shard_map/ppermute | solution.py:14
  94.0 0.9 multiply_convert_fusion.1
  95.3 1.4 collective-permute-start.11
  96.8 0.1 fusion.42
  97.1 3.0 %collective-permute-start.9 = (bf16[32,1024]{1,0:T(8,128)(2,1)S(1)}, bf16[32,1024]{1,0:T(8,128)(2,1)S(1)}, u32[]{:S(2)}, u32[]{:S(2)}) collective-permute-start(bf16[32,1024]{1,0:T(8,128)(2,1)S(1)} %maximum_maximum_fusion), channel_id=1, source_target_pairs={{0,4},{4,0},{8,12},{12,8},{1,5},{5,1},{9,13},{13,9},{2,6},{6,2},{1... | collective-permute-start | bytes 196616 | tf_op jit(solution)/shard_map/ppermute | solution.py:14
  100.1 1.3 collective-permute-done.11
  101.4 0.2 add_reduce_fusion
  101.6 1.3 collective-permute-done.10
  102.9 0.2 add_reduce_fusion.1
  103.1 0.2 add_reduce_fusion.2
  103.5 1.6 %collective-permute-start.12 = (bf16[32,3584]{1,0:T(8,128)(2,1)S(1)}, bf16[32,3584]{1,0:T(8,128)(2,1)S(1)}, u32[]{:S(2)}, u32[]{:S(2)}) collective-permute-start(bf16[32,3584]{1,0:T(8,128)(2,1)S(1)} %bitcast.183), channel_id=1, source_target_pairs={{0,2},{2,0},{1,3},{3,1},{4,6},{6,4},{5,7},{7,5},{8,10},{10,8},{9,1... | collective-permute-start | bytes 688136 | tf_op jit(solution)/shard_map/ppermute | solution.py:14
  105.2 0.1 copy.107
  105.4 4.2 %collective-permute-done.12 = bf16[32,3584]{1,0:T(8,128)(2,1)S(1)} collective-permute-done((bf16[32,3584]{1,0:T(8,128)(2,1)S(1)}, bf16[32,3584]{1,0:T(8,128)(2,1)S(1)}, u32[]{:S(2)}, u32[]{:S(2)}) %collective-permute-start.12) | collective-permute-done | bytes 229408 | tf_op jit(solution)/shard_map/ppermute | solution.py:14
  110.2 1.3 collective-permute-done.13
  111.6 0.3 fusion.12
  111.9 4.5 %fusion.7 = f32[64,1024]{1,0:T(8,128)S(1)} fusion(bf16[64,3584]{1,0:T(8,128)(2,1)S(1)} %fusion.12, bf16[1,3584,1024]{2,1,0:T(8,128)(2,1)} %param.20), kind=kOutput, calls=%fused_computation.7 | convolution fusion | flops 469762048 | bytes 8060928 | tf_op jit(solution)/shard_map/dot_general | solution.py:134
  116.4 8.1 %fusion.13 = bf16[64,3584]{1,0:T(8,128)(2,1)S(1)} fusion(bf16[1,1024,3584]{2,1,0:T(8,128)(2,1)} %param.22, bf16[64,3584]{1,0:T(8,128)(2,1)S(1)} %fusion.12, bf16[1,3584,1024]{2,1,0:T(8,128)(2,1)} %param.21, f32[64]{0:T(128)S(1)} %select_reduce_fusion, f32[64,1024]{1,0:T(8,128)S(1)} %fusion.7), kind=kOutput, calls=%fused_computation.12 | convolution fusion | flops 940376064 | bytes 15859968 | tf_op jit(solution)/shard_map/dot_general | solution.py:137
  124.5 0.3 convolution_convert_fusion
  124.8 0.2 collective-permute-start.14
  125.0 1.7 %collective-permute-done.14 = bf16[64,3584]{1,0:T(8,128)(2,1)S(1)} collective-permute-done((bf16[64,3584]{1,0:T(8,128)(2,1)S(1)}, bf16[64,3584]{1,0:T(8,128)(2,1)S(1)}, u32[]{:S(2)}, u32[]{:S(2)}) %collective-permute-start.14) | collective-permute-done | bytes 458784 | tf_op jit(solution)/shard_map/ppermute | solution.py:14
  126.7 0.3 convert_add_fusion
  126.9 0.3 reshape.395
  127.3 0.6 constant_dynamic-slice_fusion.2
  128.0 1.3 collective-permute-start.15
  129.3 1.2 collective-permute-start.16
  130.5 2.0 %collective-permute-start.17 = (bf16[64,896]{1,0:T(8,128)(2,1)S(1)}, bf16[64,896]{1,0:T(8,128)(2,1)S(1)}, u32[]{:S(2)}, u32[]{:S(2)}) collective-permute-start(bf16[64,896]{1,0:T(8,128)(2,1)S(1)} %bitcast.187), channel_id=1, source_target_pairs={{0,12},{4,8},{8,4},{12,0},{1,13},{5,9},{9,5},{13,1},{2,14},{6,10},... | collective-permute-start | bytes 344072 | tf_op jit(solution)/shard_map/ppermute | solution.py:14
  132.6 0.2 constant_dynamic-slice_fusion.3
  132.8 1.3 collective-permute-done.15
  134.1 6.7 %collective-permute-done.16 = bf16[64,896]{1,0:T(8,128)(2,1)S(1)} collective-permute-done((bf16[64,896]{1,0:T(8,128)(2,1)S(1)}, bf16[64,896]{1,0:T(8,128)(2,1)S(1)}, u32[]{:S(2)}, u32[]{:S(2)}) %collective-permute-start.16) | collective-permute-done | bytes 114720 | tf_op jit(solution)/shard_map/ppermute | solution.py:14
  140.9 1.6 %collective-permute-start.18 = (bf16[2,32,896]{2,1,0:T(8,128)(2,1)S(1)}, bf16[2,32,896]{2,1,0:T(8,128)(2,1)S(1)}, u32[]{:S(2)}, u32[]{:S(2)}) collective-permute-start(bf16[2,32,896]{2,1,0:T(8,128)(2,1)S(1)} %fusion.57), channel_id=1, source_target_pairs={{0,2},{2,0},{1,3},{3,1},{4,6},{6,4},{5,7},{7,5},{8,10},{10,8},{9,1... | collective-permute-start | bytes 344072 | tf_op jit(solution)/shard_map/ppermute | solution.py:14
  142.5 3.3 %collective-permute-done.18 = bf16[2,32,896]{2,1,0:T(8,128)(2,1)S(1)} collective-permute-done((bf16[2,32,896]{2,1,0:T(8,128)(2,1)S(1)}, bf16[2,32,896]{2,1,0:T(8,128)(2,1)S(1)}, u32[]{:S(2)}, u32[]{:S(2)}) %collective-permute-start.18) | collective-permute-done | bytes 114720 | tf_op jit(solution)/shard_map/ppermute | solution.py:14
  146.0 1.3 collective-permute-done.19
  147.3 0.7 copy.112
  (68 shorter events, 2.9 us)
Async XLA Ops:
  0.0 6.8 %copy-start = (bf16[32,32,576]{2,1,0:T(8,128)(2,1)S(1)}, bf16[32,32,576]{2,1,0:T(8,128)(2,1)}, u32[]{:S(2)}) copy-start(bf16[32,32,576]{2,1,0:T(8,128)(2,1)} %param.13) | copy-start | bytes 3538948
  2.0 27.6 %collective-permute-start.1 = (bf16[16,512,32]{1,2,0:T(8,128)(2,1)}, bf16[16,512,32]{1,2,0:T(8,128)(2,1)}, u32[]{:S(2)}, u32[]{:S(2)}) collective-permute-start(bf16[16,512,32]{1,2,0:T(8,128)(2,1)} %dynamic-slice_bitcast_fusion), channel_id=1, source_target_pairs={{0,8},{4,12},{8,0},{12,4},{1,9},{5,13},{9,1},{13,5},{2,10},{6,14},... | collective-permute-start | bytes 1572872 | tf_op jit(solution)/shard_map/ppermute | solution.py:14
  18.2 33.7 %collective-permute-start = (bf16[32,32,512]{2,1,0:T(8,128)(2,1)S(1)}, bf16[32,32,512]{2,1,0:T(8,128)(2,1)S(1)}, u32[]{:S(2)}, u32[]{:S(2)}) collective-permute-start(bf16[32,32,512]{2,1,0:T(8,128)(2,1)S(1)} %divide_convert_fusion), channel_id=1, source_target_pairs={{0,4},{4,0},{8,12},{12,8},{1,5},{5,1},{9,13},{13,9},{2,6},{6,2},{1... | collective-permute-start | bytes 3145736 | tf_op jit(solution)/shard_map/ppermute | solution.py:14
  29.6 13.3 %collective-permute-start.2 = (bf16[16,512,32]{1,2,0:T(8,128)(2,1)}, bf16[16,512,32]{1,2,0:T(8,128)(2,1)}, u32[]{:S(2)}, u32[]{:S(2)}) collective-permute-start(bf16[16,512,32]{1,2,0:T(8,128)(2,1)} %collective-permute-done.1), channel_id=1, source_target_pairs={{0,16},{16,0},{1,17},{17,1},{2,18},{18,2},{3,19},{19,3},{4,20},{20... | collective-permute-start | bytes 1572872 | tf_op jit(solution)/shard_map/ppermute | solution.py:14
  53.4 14.8 %collective-permute-start.3 = (bf16[64,32,32]{0,2,1:T(8,128)(2,1)S(1)}, bf16[64,32,32]{0,2,1:T(8,128)(2,1)S(1)}, u32[]{:S(2)}, u32[]{:S(2)}) collective-permute-start(bf16[64,32,32]{0,2,1:T(8,128)(2,1)S(1)} %fusion.30), channel_id=1, source_target_pairs={{0,8},{4,12},{8,0},{12,4},{1,9},{5,13},{9,1},{13,5},{2,10},{6,14},... | collective-permute-start | bytes 393224 | tf_op jit(solution)/shard_map/ppermute | solution.py:14
  69.1 9.2 %copy-start.4 = (s32[128,2]{0,1:T(2,128)S(1)}, s32[128,2]{0,1:T(2,128)}, u32[]{:S(2)}) copy-start(s32[128,2]{0,1:T(2,128)} %param.23) | copy-start | bytes 3076
  69.1 9.2 %copy-start.5 = (s32[8]{0:T(128)S(1)}, s32[8]{0:T(128)}, u32[]{:S(2)}) copy-start(s32[8]{0:T(128)} %param.25) | copy-start | bytes 100
  69.1 24.9 %copy-start.2 = (f32[896]{0:T(1024)S(1)}, f32[896]{0:T(1024)}, u32[]{:S(2)}) copy-start(f32[896]{0:T(1024)} %param.19) | copy-start | bytes 10756
  73.4 36.4 %copy-start.3 = (f32[128,2]{0,1:T(2,128)S(1)}, f32[128,2]{0,1:T(2,128)}, u32[]{:S(2)}) copy-start(f32[128,2]{0,1:T(2,128)} %param.24) | copy-start | bytes 3076
  73.4 2.0 %collective-permute-start.4 = (bf16[2,32,3584]{2,1,0:T(8,128)(2,1)S(1)}, bf16[2,32,3584]{2,1,0:T(8,128)(2,1)}, u32[]{:S(2)}, u32[]{:S(2)}) collective-permute-start(bf16[2,32,3584]{2,1,0:T(8,128)(2,1)S(1)} %fusion.51), channel_id=1, source_target_pairs={{0,1},{1,0},{2,3},{3,2},{4,5},{5,4},{6,7},{7,6},{8,9},{9,8},{10,11... | collective-permute-start | bytes 1376264 | tf_op jit(solution)/shard_map/ppermute | solution.py:14
  76.6 7.7 %collective-permute-start.5 = (bf16[32,3584]{1,0:T(8,128)(2,1)S(1)}, bf16[32,3584]{1,0:T(8,128)(2,1)S(1)}, u32[]{:S(2)}, u32[]{:S(2)}) collective-permute-start(bf16[32,3584]{1,0:T(8,128)(2,1)S(1)} %fusion.58), channel_id=1, source_target_pairs={{0,2},{2,0},{1,3},{3,1},{4,6},{6,4},{5,7},{7,5},{8,10},{10,8},{9,1... | collective-permute-start | bytes 688136 | tf_op jit(solution)/shard_map/ppermute | solution.py:14
  84.9 4.7 %collective-permute-start.6 = (bf16[32,896]{1,0:T(8,128)(2,1)S(1)}, bf16[32,896]{1,0:T(8,128)(2,1)S(1)}, u32[]{:S(2)}, u32[]{:S(2)}) collective-permute-start(bf16[32,896]{1,0:T(8,128)(2,1)S(1)} %bitcast.188), channel_id=1, source_target_pairs={{0,4},{4,0},{8,12},{12,8},{1,5},{5,1},{9,13},{13,9},{2,6},{6,2},{1... | collective-permute-start | bytes 172040 | tf_op jit(solution)/shard_map/ppermute | solution.py:14
  85.0 5.9 %collective-permute-start.7 = (bf16[32,896]{1,0:T(8,128)(2,1)S(1)}, bf16[32,896]{1,0:T(8,128)(2,1)S(1)}, u32[]{:S(2)}, u32[]{:S(2)}) collective-permute-start(bf16[32,896]{1,0:T(8,128)(2,1)S(1)} %bitcast.189), channel_id=1, source_target_pairs={{0,8},{4,12},{8,0},{12,4},{1,9},{5,13},{9,1},{13,5},{2,10},{6,14},... | collective-permute-start | bytes 172040 | tf_op jit(solution)/shard_map/ppermute | solution.py:14
  88.0 6.0 %collective-permute-start.8 = (bf16[32,896]{1,0:T(8,128)(2,1)S(1)}, bf16[32,896]{1,0:T(8,128)(2,1)S(1)}, u32[]{:S(2)}, u32[]{:S(2)}) collective-permute-start(bf16[32,896]{1,0:T(8,128)(2,1)S(1)} %bitcast.190), channel_id=1, source_target_pairs={{0,12},{4,8},{8,4},{12,0},{1,13},{5,9},{9,5},{13,1},{2,14},{6,10},... | collective-permute-start | bytes 172040 | tf_op jit(solution)/shard_map/ppermute | solution.py:14
  95.3 6.1 %collective-permute-start.11 = (bf16[32,1024]{1,0:T(8,128)(2,1)S(1)}, bf16[32,1024]{1,0:T(8,128)(2,1)S(1)}, u32[]{:S(2)}, u32[]{:S(2)}) collective-permute-start(bf16[32,1024]{1,0:T(8,128)(2,1)S(1)} %maximum_maximum_fusion), channel_id=1, source_target_pairs={{0,12},{4,8},{8,4},{12,0},{1,13},{5,9},{9,5},{13,1},{2,14},{6,10},... | collective-permute-start | bytes 196616 | tf_op jit(solution)/shard_map/ppermute | solution.py:14
  97.1 5.8 %collective-permute-start.10 = (bf16[32,1024]{1,0:T(8,128)(2,1)S(1)}, bf16[32,1024]{1,0:T(8,128)(2,1)S(1)}, u32[]{:S(2)}, u32[]{:S(2)}) collective-permute-start(bf16[32,1024]{1,0:T(8,128)(2,1)S(1)} %maximum_maximum_fusion), channel_id=1, source_target_pairs={{0,8},{4,12},{8,0},{12,4},{1,9},{5,13},{9,1},{13,5},{2,10},{6,14},... | collective-permute-start | bytes 196616 | tf_op jit(solution)/shard_map/ppermute | solution.py:14
  97.1 6.0 %collective-permute-start.9 = (bf16[32,1024]{1,0:T(8,128)(2,1)S(1)}, bf16[32,1024]{1,0:T(8,128)(2,1)S(1)}, u32[]{:S(2)}, u32[]{:S(2)}) collective-permute-start(bf16[32,1024]{1,0:T(8,128)(2,1)S(1)} %maximum_maximum_fusion), channel_id=1, source_target_pairs={{0,4},{4,0},{8,12},{12,8},{1,5},{5,1},{9,13},{13,9},{2,6},{6,2},{1... | collective-permute-start | bytes 196616 | tf_op jit(solution)/shard_map/ppermute | solution.py:14
  103.5 6.1 %collective-permute-start.12 = (bf16[32,3584]{1,0:T(8,128)(2,1)S(1)}, bf16[32,3584]{1,0:T(8,128)(2,1)S(1)}, u32[]{:S(2)}, u32[]{:S(2)}) collective-permute-start(bf16[32,3584]{1,0:T(8,128)(2,1)S(1)} %bitcast.183), channel_id=1, source_target_pairs={{0,2},{2,0},{1,3},{3,1},{4,6},{6,4},{5,7},{7,5},{8,10},{10,8},{9,1... | collective-permute-start | bytes 688136 | tf_op jit(solution)/shard_map/ppermute | solution.py:14
  109.7 1.9 %collective-permute-start.13 = (bf16[2,32,3584]{2,1,0:T(8,128)(2,1)S(1)}, bf16[2,32,3584]{2,1,0:T(8,128)(2,1)S(1)}, u32[]{:S(2)}, u32[]{:S(2)}) collective-permute-start(bf16[2,32,3584]{2,1,0:T(8,128)(2,1)S(1)} %get-tuple-element.17), channel_id=1, source_target_pairs={{0,1},{1,0},{2,3},{3,2},{4,5},{5,4},{6,7},{7,6},{8,9},{9,8},{10,11... | collective-permute-start | bytes 1376264 | tf_op jit(solution)/shard_map/ppermute | solution.py:14
  116.4 31.7 %copy-start.1 = (bf16[32,32,576]{2,1,0:T(8,128)(2,1)S(1)}, bf16[32,32,576]{2,1,0:T(8,128)(2,1)}, u32[]{:S(2)}) copy-start(bf16[32,32,576]{2,1,0:T(8,128)(2,1)} %param.13) | copy-start | bytes 3538948
  124.8 1.9 %collective-permute-start.14 = (bf16[64,3584]{1,0:T(8,128)(2,1)S(1)}, bf16[64,3584]{1,0:T(8,128)(2,1)S(1)}, u32[]{:S(2)}, u32[]{:S(2)}) collective-permute-start(bf16[64,3584]{1,0:T(8,128)(2,1)S(1)} %convolution_convert_fusion), channel_id=1, source_target_pairs={{0,1},{1,0},{2,3},{3,2},{4,5},{5,4},{6,7},{7,6},{8,9},{9,8},{10,11... | collective-permute-start | bytes 1376264 | tf_op jit(solution)/shard_map/ppermute | solution.py:14
  128.0 6.1 %collective-permute-start.15 = (bf16[64,896]{1,0:T(8,128)(2,1)S(1)}, bf16[64,896]{1,0:T(8,128)(2,1)S(1)}, u32[]{:S(2)}, u32[]{:S(2)}) collective-permute-start(bf16[64,896]{1,0:T(8,128)(2,1)S(1)} %bitcast.185), channel_id=1, source_target_pairs={{0,4},{4,0},{8,12},{12,8},{1,5},{5,1},{9,13},{13,9},{2,6},{6,2},{1... | collective-permute-start | bytes 344072 | tf_op jit(solution)/shard_map/ppermute | solution.py:14
  129.3 11.5 %collective-permute-start.16 = (bf16[64,896]{1,0:T(8,128)(2,1)S(1)}, bf16[64,896]{1,0:T(8,128)(2,1)S(1)}, u32[]{:S(2)}, u32[]{:S(2)}) collective-permute-start(bf16[64,896]{1,0:T(8,128)(2,1)S(1)} %bitcast.186), channel_id=1, source_target_pairs={{0,8},{4,12},{8,0},{12,4},{1,9},{5,13},{9,1},{13,5},{2,10},{6,14},... | collective-permute-start | bytes 344072 | tf_op jit(solution)/shard_map/ppermute | solution.py:14
  130.5 10.2 %collective-permute-start.17 = (bf16[64,896]{1,0:T(8,128)(2,1)S(1)}, bf16[64,896]{1,0:T(8,128)(2,1)S(1)}, u32[]{:S(2)}, u32[]{:S(2)}) collective-permute-start(bf16[64,896]{1,0:T(8,128)(2,1)S(1)} %bitcast.187), channel_id=1, source_target_pairs={{0,12},{4,8},{8,4},{12,0},{1,13},{5,9},{9,5},{13,1},{2,14},{6,10},... | collective-permute-start | bytes 344072 | tf_op jit(solution)/shard_map/ppermute | solution.py:14
  140.9 4.9 %collective-permute-start.18 = (bf16[2,32,896]{2,1,0:T(8,128)(2,1)S(1)}, bf16[2,32,896]{2,1,0:T(8,128)(2,1)S(1)}, u32[]{:S(2)}, u32[]{:S(2)}) collective-permute-start(bf16[2,32,896]{2,1,0:T(8,128)(2,1)S(1)} %fusion.57), channel_id=1, source_target_pairs={{0,2},{2,0},{1,3},{3,1},{4,6},{6,4},{5,7},{7,5},{8,10},{10,8},{9,1... | collective-permute-start | bytes 344072 | tf_op jit(solution)/shard_map/ppermute | solution.py:14
  145.9 1.4 collective-permute-start.19
